TPU v7x, 32 devices: a whole 2x2x4 slice. The times are simulated.
32 devices in a mesh: kpt: 1, ga: 32 (over z, y, x, core).
Axes of the slice: x: 2, y: 2, z: 4, core: 2. Of those that a mesh axis runs over, the one named last changes fastest.
Arguments:
- orbitals: float32 [2, 1024, 131072], P(None, 'kpt', 'ga'), may hold values from -6 to 6
- coeff_cells: int32 [131072], P('ga'), may hold values from -1 to 2097151, as said below
- potential: float32 [128, 128, 128], P('ga'), may hold values from -6 to 6
Outputs:
- applied: float32 [2, 1, 131072], P(None, 'kpt', 'ga')
- subspace: float32 [1024, 2, 1], P('ga', None, 'kpt')
Inputs may be any that keep to these rules, and one draw needn't show every extreme that they name: `coeff_cells`: each block of 4096 entries (one device's) lists whole columns of cells (cells with the same first two coordinates) one after another, each column's cells in rising third coordinate, and then -1 in its remaining slots. The cells listed over all blocks are exactly the cells with f(a)^2 + f(b)^2 + f(c)^2 <= 30^2, each once. The numbers of columns of two blocks differ by one at most.
All inputs are finite; a program needn't handle non-finite values.
Results may differ from a plain program's by a relative error of at most 0.0003.
Values sent between devices are 32-bit elements; how exact they have to be, the bound alone decides.
A program may use at most 128 MiB of HBM per device.

v0:
```python
import functools

import jax
import jax.numpy as jnp
import ml_dtypes
import numpy as np
from jax import lax
from jax.experimental import pallas as pl
from jax.experimental.pallas import tpu as pltpu
from jax.sharding import PartitionSpec as P

RADIUS = 30
BF = jnp.bfloat16
F32 = jnp.float32
LANES = 128
NN = (((1,), (0,)), ((), ()))
NT = (((1,), (1,)), ((), ()))


def split_np(table):
    high = table.astype(np.float32).astype(ml_dtypes.bfloat16)
    low = (table - high.astype(np.float64)).astype(np.float32).astype(ml_dtypes.bfloat16)
    return high, low


def stack_np(table, axis):
    high, low = split_np(table)
    return np.concatenate([high, high, low], axis=axis)


def phases(extent, half):
    index = np.arange(half)
    freq = np.where(index < half // 2, index, index - half)
    angle = 2.0 * np.pi * ((np.arange(extent)[:, None] * freq[None, :]) % extent) / extent
    return np.cos(angle), np.sin(angle)


@functools.lru_cache(None)
def tables(extent, count, rows_msg, sub_rows):
    half = extent // 2
    layers = extent // count
    cos, sin = phases(extent, half)
    first = np.zeros((count, rows_msg, 2 * half))
    last = np.zeros((2 * half, count, rows_msg))
    for l in range(layers):
        z = np.arange(count) * layers + l
        first[:, l, :half], first[:, l, half:] = cos[z], -sin[z]
        first[:, layers + l, :half], first[:, layers + l, half:] = sin[z], cos[z]
        last[:half, :, l], last[:half, :, layers + l] = cos[z].T, sin[z].T
        last[half:, :, l], last[half:, :, layers + l] = -sin[z].T, cos[z].T
    first = first.reshape(count * rows_msg, 2 * half)
    last = last.reshape(2 * half, count * rows_msg) / float(extent) ** 3
    up_a = np.block([[cos, -sin], [sin, cos]])
    up_b = np.concatenate([cos.T, sin.T], axis=1)
    down_b = np.block([[cos, -sin], [sin, cos]])
    down_a = np.concatenate([cos.T, sin.T], axis=0)
    index = np.arange(count * sub_rows)
    fold = np.zeros((2, count * sub_rows, LANES), np.float32)
    fold[0, index, index % sub_rows] = 1.0
    fold[1, index, sub_rows + index % sub_rows] = 1.0
    up_b_high, up_b_low = split_np(up_b)
    return (
        stack_np(first, 1),
        stack_np(up_a, 1),
        np.stack([up_b_high, up_b_low]),
        stack_np(down_b, 0),
        stack_np(down_a, 1),
        stack_np(last, 1),
        fold.astype(ml_dtypes.bfloat16),
    )


def dot(left, right, dims=NN):
    return lax.dot_general(left, right, dims, preferred_element_type=F32)


def split(values):
    high = values.astype(BF)
    return high, (values - high.astype(F32)).astype(BF)


def stacked(values, axis):
    high, low = split(values)
    return jnp.concatenate([high, low, high], axis=axis)


def signed(values, extent):
    return jnp.where(values < extent // 2, values, values - extent)


def kernel(
    count, layers, extent, rows_msg, group,
    cells_hbm, pot_hbm, first_hbm, up_a_hbm, up_b_hbm, down_b_hbm, down_a_hbm, last_hbm, fold_hbm,
    orb_hbm, applied_ref, sub_ref,
    cells_ref, pot_ref, first_ref, up_a_ref, up_b_ref, down_b_ref, down_a_ref, last_ref, fold_ref,
    orb, spread, place, cols, ids_out, ids_out2, ids_in, msg, arrived, pot_out, pot_in,
    slab, pick_b, grid, freq, back, back_in, sums, sub_out, sub_in, kin, colrow, space,
    win_sem, orb_sem, load_sem, send_sem, recv_sem, ids_sem, msg_sem,
):
    me = lax.axis_index("ga")
    half = extent // 2
    slots = orb.shape[2]
    blocks = slots // LANES
    bands_all = orb.shape[1]
    sub_rows = bands_all // count
    parts = 2 * layers

    head = pltpu.make_async_copy(orb_hbm.at[:, 0:8, :], orb.at[:, 0:8, :], win_sem)
    head.start()
    sources = (
        cells_hbm, first_hbm, pot_hbm, up_a_hbm, up_b_hbm, down_b_hbm, down_a_hbm, last_hbm, fold_hbm
    )
    targets = (
        cells_ref, first_ref, pot_ref, up_a_ref, up_b_ref, down_b_ref, down_a_ref, last_ref, fold_ref
    )
    loads = [
        pltpu.make_async_copy(source, target, load_sem.at[i])
        for i, (source, target) in enumerate(zip(sources, targets))
    ]
    load_cells, load_first, load_pot, load_up_a, load_up_b, load_down_b, load_down_a, load_last, load_fold = loads
    for load in loads:
        load.start()

    barrier = pltpu.get_barrier_semaphore()

    def greet(i, carry):
        other = lax.rem(me + i, count)
        pl.semaphore_signal(barrier, inc=1, device_id={"ga": other})
        return carry

    lax.fori_loop(1, count, greet, 0)
    rest = pltpu.make_async_copy(orb_hbm.at[:, 8:, :], orb.at[:, 8:, :], orb_sem)
    rest.start()
    groups = count // group
    my_group = me // group

    def exchange(source, target, phase, landed):
        own = pltpu.make_async_copy(source.at[me], target.at[me], landed)
        own.start()

        def send(i, carry):
            other = lax.rem(me + i, count)
            pltpu.make_async_remote_copy(
                src_ref=source.at[other],
                dst_ref=target.at[me],
                send_sem=send_sem.at[phase],
                recv_sem=landed,
                device_id={"ga": other},
            ).start()
            return carry

        lax.fori_loop(1, count, send, 0)

    def arrive(target, phase):
        pltpu.make_async_copy(target, target, recv_sem.at[phase]).wait()

    def sent(source, phase):
        view = source.at[pl.ds(0, count - 1)]
        pltpu.make_async_copy(view, view, send_sem.at[phase]).wait()

    load_cells.wait()
    cells = cells_ref[...]
    live = cells >= 0
    column = jnp.right_shift(cells, extent.bit_length() - 1)
    rolled = pltpu.roll(column, 1, 1)
    lane = lax.broadcasted_iota(jnp.int32, cells.shape, 1)
    row = lax.broadcasted_iota(jnp.int32, cells.shape, 0)
    earlier = jnp.where(lane == 0, pltpu.roll(rolled, 1, 0), rolled)
    earlier = jnp.where((lane == 0) & (row == 0), -1, earlier)
    starts = live & (column != earlier)
    flags = starts.astype(F32).astype(BF)
    sq = lambda axis: lax.broadcasted_iota(jnp.int32, (LANES, LANES), axis)
    upper = (sq(0) <= sq(1)).astype(F32).astype(BF)
    inner = dot(flags, upper)
    totals = dot(flags, jnp.ones((LANES, LANES), BF))
    below = lax.broadcasted_iota(jnp.int32, (blocks, blocks), 1) < lax.broadcasted_iota(
        jnp.int32, (blocks, blocks), 0
    )
    outer = dot(below.astype(F32).astype(BF), totals.astype(BF))
    local = (inner + outer - 1.0).astype(jnp.int32)
    local = jnp.where(live, local, -1)
    safe = jnp.where(live, cells, 0)
    plane_c = safe % extent
    plane_b = safe // extent % extent
    plane_a = safe // (extent * extent)
    fa, fb, fc = signed(plane_a, extent), signed(plane_b, extent), signed(plane_c, extent)
    kinetic = (fa * fa + fb * fb + fc * fc).astype(F32) / (RADIUS * RADIUS)
    kin[...] = jnp.where(live, kinetic, 0.0)
    colrow[0] = local
    colrow[1] = plane_c % half
    colrow[2] = jnp.where(starts, plane_a % half, 0)
    colrow[3] = jnp.where(starts, plane_b % half, 0)

    head.wait()
    sub_half = lax.broadcasted_iota(jnp.int32, (half, LANES), 0)
    sub_full = lax.broadcasted_iota(jnp.int32, (LANES, LANES), 0)
    sub_ids = lax.broadcasted_iota(jnp.int32, (16, LANES), 0)

    def fill(r, carry):
        span = pl.ds(pl.multiple_of(r * LANES, LANES), LANES)
        mine = colrow[0, pl.ds(r, 1), :]
        depth = colrow[1, pl.ds(r, 1), :]
        is_a = colrow[2, pl.ds(r, 1), :].astype(F32)
        is_b = colrow[3, pl.ds(r, 1), :].astype(F32)
        place[0:LANES, span] = jnp.where(sub_full == mine, 1.0, 0.0).astype(BF)
        at_depth = sub_half == depth
        for part in range(2):
            values = orb[part, 0:1, span]
            high, low = split(values)
            spread[2 * part * half : (2 * part + 1) * half, span] = jnp.where(
                at_depth, high.astype(F32), 0.0
            ).astype(BF)
            spread[(2 * part + 1) * half : (2 * part + 2) * half, span] = jnp.where(
                at_depth, low.astype(F32), 0.0
            ).astype(BF)
        tail = jnp.where(sub_ids == 0, is_a, jnp.where(sub_ids == 1, is_b, 0.0))
        spread[4 * half : 4 * half + 16, span] = tail.astype(BF)
        return carry

    lax.fori_loop(0, blocks, fill, 0)
    sticks = dot(spread[...], place[...], NT)
    code = sticks[4 * half : 4 * half + 1] * half + sticks[4 * half + 1 : 4 * half + 2]

    def copy_ids(d, carry):
        ids_out[d] = code
        return carry

    lax.fori_loop(0, count, copy_ids, 0)
    both = jnp.concatenate(
        [
            sticks[0:half] + sticks[half : 2 * half],
            sticks[2 * half : 3 * half] + sticks[3 * half : 4 * half],
        ],
        axis=0,
    )
    load_first.wait()
    msg[...] = dot(first_ref[...], stacked(both, 0)).reshape(count, rows_msg, LANES)
    pl.semaphore_wait(barrier, count - 1)
    exchange(ids_out, ids_in, 0, ids_sem.at[my_group])
    exchange(msg, arrived, 1, msg_sem.at[my_group])

    load_pot.wait()
    for a in range(layers):
        turned = jnp.transpose(pot_ref[a])
        for d in range(count):
            pot_out[d, a * layers : (a + 1) * layers, :] = turned[d * layers : (d + 1) * layers]
    exchange(pot_out, pot_in, 2, recv_sem.at[2])

    grid[...] = jnp.zeros_like(grid)

    def gather_group(step, carry):
        g = lax.rem(my_group + step, groups)
        ids_view = ids_in.at[pl.ds(g * group, group)]
        pltpu.make_async_copy(ids_view, ids_view, ids_sem.at[g]).wait()
        msg_view = arrived.at[pl.ds(g * group, group)]
        pltpu.make_async_copy(msg_view, msg_view, msg_sem.at[g]).wait()
        for k in range(group):
            d = g * group + k
            number = ids_in[d].astype(jnp.int32)
            in_a = sub_half == number // half
            span = pl.ds(k * LANES, LANES)
            pick_b[:, span] = jnp.where(sub_half == number % half, 1.0, 0.0).astype(BF)
            tile = arrived[d]
            high, low = split(tile)
            high, low = high.astype(F32), low.astype(F32)
            for p in range(parts):
                slab[2 * p * half : (2 * p + 1) * half, span] = jnp.where(
                    in_a, high[p : p + 1], 0.0
                ).astype(BF)
                slab[(2 * p + 1) * half : (2 * p + 2) * half, span] = jnp.where(
                    in_a, low[p : p + 1], 0.0
                ).astype(BF)
        grid[...] += dot(slab[...], pick_b[...], NT)
        return carry

    lax.fori_loop(0, groups, gather_group, 0)
    load_up_a.wait()
    load_up_b.wait()
    load_down_b.wait()
    load_down_a.wait()

    for l in range(layers):
        pair = []
        for p in (l, layers + l):
            base = 2 * p * half
            pair.append(grid[base : base + half] + grid[base + half : base + 2 * half])
        lifted = dot(up_a_ref[...], stacked(jnp.concatenate(pair, axis=0), 0))
        high, low = split(lifted)
        full = dot(high, up_b_ref[0]) + dot(low, up_b_ref[0]) + dot(high, up_b_ref[1])
        space[0, l] = full[:extent, :extent] - full[extent:, extent:]
        space[1, l] = full[:extent, extent:] + full[extent:, :extent]

    arrive(pot_in, 2)
    for l in range(layers):
        planes = [pot_in[d, a * layers + l : a * layers + l + 1, :] for d in range(count) for a in range(layers)]
        local_pot = jnp.concatenate(planes, axis=0)
        field = jnp.concatenate([space[0, l] * local_pot, space[1, l] * local_pot], axis=1)
        fallen = dot(stacked(field, 1), down_b_ref[...])
        product = dot(down_a_ref[...], stacked(fallen, 0))
        swap = pltpu.roll(product[half:], half, 1)
        lane_half = lax.broadcasted_iota(jnp.int32, (half, 2 * half), 1)
        total = product[:half] + jnp.where(lane_half < half, swap, -swap)
        high, low = split(total)
        freq[l * half : (l + 1) * half, :] = jnp.concatenate([high, low], axis=1)

    def take_columns(d):
        number = ids_in[d].astype(jnp.int32)
        in_a = sub_half == number // half
        in_b = jnp.where(sub_half == number % half, 1.0, 0.0).astype(BF)
        none = jnp.zeros_like(in_b)
        upper_rows = jnp.concatenate([in_b, none], axis=1)
        lower_rows = jnp.concatenate([none, in_b], axis=1)
        picker = jnp.concatenate([upper_rows, lower_rows, upper_rows, lower_rows], axis=0)
        found = dot(freq[...], picker)
        rows = []
        for part in range(2):
            for l in range(layers):
                block = found[l * half : (l + 1) * half, part * LANES : (part + 1) * LANES]
                rows.append(jnp.sum(jnp.where(in_a, block, 0.0), axis=0, keepdims=True))
        if rows_msg > parts:
            rows.append(jnp.zeros((rows_msg - parts, LANES), F32))
        return jnp.concatenate(rows, axis=0)

    wide = 4

    def give(index):
        other = lax.rem(me + index, count)
        pltpu.make_async_remote_copy(
            src_ref=back.at[other],
            dst_ref=back_in.at[me],
            send_sem=send_sem.at[3],
            recv_sem=recv_sem.at[3],
            device_id={"ga": other},
        ).start()

    def take_some(i, carry):
        @pl.when(i > 0)
        def _():
            for k in range(wide):
                give((i - 1) * wide + k + 1)

        who = [lax.rem(me + i * wide + k + 1, count) for k in range(wide)]
        tiles = [take_columns(d) for d in who]
        for d, tile in zip(who, tiles):
            back[d] = tile
        return carry

    lax.fori_loop(0, count // wide, take_some, 0)
    for k in range(wide - 1):
        give(count - wide + k + 1)
    pltpu.make_async_copy(back.at[me], back_in.at[me], recv_sem.at[3]).start()
    load_last.wait()
    load_fold.wait()
    arrive(back_in, 3)

    final = dot(last_ref[...], stacked(back_in[...].reshape(count * rows_msg, LANES), 0))
    high, low = split(final)
    final_cat = jnp.concatenate([high, low], axis=1)
    place_rows = jnp.concatenate([place[...], place[...]], axis=0)
    spread_back = dot(final_cat, place_rows)
    for r in range(blocks):
        at_depth = sub_half == colrow[1, r : r + 1, :]
        span = slice(r * LANES, (r + 1) * LANES)
        k_row = kin[r : r + 1, :]
        for part in range(2):
            block = spread_back[part * half : (part + 1) * half, span]
            value = jnp.sum(jnp.where(at_depth, block, 0.0), axis=0, keepdims=True)
            applied_ref[part, r : r + 1, :] = value + k_row * orb[part, 0:1, span]

    rest.wait()
    tile_rows = 64

    def rows_of(t, carry):
        at = pl.ds(pl.multiple_of(t * tile_rows, tile_rows), tile_rows)
        acc_re = jnp.zeros((tile_rows, LANES), F32)
        acc_im = jnp.zeros((tile_rows, LANES), F32)
        for r in range(blocks):
            span = slice(r * LANES, (r + 1) * LANES)
            a_re = applied_ref[0, r : r + 1, :]
            a_im = applied_ref[1, r : r + 1, :]
            o_re = orb[0, at, span]
            o_im = orb[1, at, span]
            acc_re = acc_re + (o_re * a_re + o_im * a_im)
            acc_im = acc_im + (o_re * a_im - o_im * a_re)
        sums[0, at, :] = acc_re
        sums[1, at, :] = acc_im
        return carry

    lax.fori_loop(0, bands_all // tile_rows, rows_of, 0)
    ones = jnp.ones((16, LANES), BF)
    owner = lax.broadcasted_iota(jnp.int32, (count, bands_all), 1) // sub_rows
    is_owner = owner == lax.broadcasted_iota(jnp.int32, (count, bands_all), 0)
    folded = jnp.zeros((count, LANES), F32)
    for part in range(2):
        high, low = split(sums[part])
        line = (dot(ones, high, NT) + dot(ones, low, NT))[0:1]
        high, low = split(jnp.where(is_owner, line, 0.0))
        folded = folded + dot(high, fold_ref[part]) + dot(low, fold_ref[part])
    for d in range(count):
        sub_out[d] = folded[d : d + 1] * (1.0 / (slots * count))
    exchange(sub_out, sub_in, 4, recv_sem.at[4])
    arrive(sub_in, 4)
    total = jnp.sum(sub_in[...], axis=0)
    sub_ref[0] = total[:, :sub_rows]
    sub_ref[1] = total[:, sub_rows : 2 * sub_rows]
    sent(ids_out, 0)
    sent(msg, 1)
    sent(pot_out, 2)
    sent(back, 3)
    sent(sub_out, 4)


def local(orbitals, coeff_cells, potential):
    count = lax.axis_size("ga")
    extent = potential.shape[1]
    layers = extent // count
    half = extent // 2
    bands_all, slots = orbitals.shape[1], orbitals.shape[2]
    blocks = slots // LANES
    parts = 2 * layers
    rows_msg = -(-parts // 8) * 8
    sub_rows = bands_all // count
    group = 8
    constants = [jnp.asarray(t) for t in tables(extent, count, rows_msg, sub_rows)]
    vmem = pl.BlockSpec(memory_space=pltpu.VMEM)
    staged = [(blocks, LANES), (layers, extent, extent)] + [t.shape for t in constants]
    kinds = [jnp.int32, F32] + [BF] * len(constants)
    scratch = [pltpu.VMEM(shape, kind) for shape, kind in zip(staged, kinds)] + [
        pltpu.VMEM((2, bands_all, slots), F32),
        pltpu.VMEM((4 * half + 16, slots), BF),
        pltpu.VMEM((LANES, slots), BF),
        pltpu.VMEM((8, LANES), F32),
        pltpu.VMEM((count, 1, LANES), F32),
        pltpu.VMEM((8, LANES), F32),
        pltpu.VMEM((count, 1, LANES), F32),
        pltpu.VMEM((count, rows_msg, LANES), F32),
        pltpu.VMEM((count, rows_msg, LANES), F32),
        pltpu.VMEM((count, layers * layers, LANES), F32),
        pltpu.VMEM((count, layers * layers, LANES), F32),
        pltpu.VMEM((2 * parts * half, group * LANES), BF),
        pltpu.VMEM((half, group * LANES), BF),
        pltpu.VMEM((2 * parts * half, half), F32),
        pltpu.VMEM((layers * half, 4 * half), BF),
        pltpu.VMEM((count, rows_msg, LANES), F32),
        pltpu.VMEM((count, rows_msg, LANES), F32),
        pltpu.VMEM((2, bands_all, LANES), F32),
        pltpu.VMEM((count, 1, LANES), F32),
        pltpu.VMEM((count, 1, LANES), F32),
        pltpu.VMEM((blocks, LANES), F32),
        pltpu.VMEM((4, blocks, LANES), jnp.int32),
        pltpu.VMEM((2, layers, extent, extent), F32),
        pltpu.SemaphoreType.DMA,
        pltpu.SemaphoreType.DMA,
        pltpu.SemaphoreType.DMA((len(staged),)),
        pltpu.SemaphoreType.DMA((5,)),
        pltpu.SemaphoreType.DMA((5,)),
        pltpu.SemaphoreType.DMA((count // group,)),
        pltpu.SemaphoreType.DMA((count // group,)),
    ]
    applied, sub = pl.pallas_call(
        functools.partial(kernel, count, layers, extent, rows_msg, group),
        out_shape=(
            jax.ShapeDtypeStruct((2, blocks, LANES), F32),
            jax.ShapeDtypeStruct((2, 1, sub_rows), F32),
        ),
        in_specs=[pl.BlockSpec(memory_space=pl.ANY)] * (3 + len(constants)),
        out_specs=(vmem, vmem),
        scratch_shapes=scratch,
        compiler_params=pltpu.CompilerParams(
            collective_id=0, has_side_effects=True, vmem_limit_bytes=60 * 1024 * 1024
        ),
    )(coeff_cells.reshape(blocks, LANES), potential, *constants, orbitals)
    applied = applied.reshape(2, 1, slots)
    subspace = jnp.transpose(sub, (2, 0, 1))
    return applied, subspace


def solution(mesh):
    in_specs = (P(None, "kpt", "ga"), P("ga"), P("ga", None, None))
    out_specs = (P(None, "kpt", "ga"), P("ga", None, "kpt"))
    return jax.shard_map(local, mesh=mesh, in_specs=in_specs, out_specs=out_specs, check_vma=False)
```

profile of v0, /device:TPU:0, one launch (start us, length us, event | category | flops | bytes accessed | tf_op | source)
XLA Modules:
  0.0 42.0 jit_solution(16276059849146432068)
XLA Ops:
  0.6 38.8 %shard_map.113 = (f32[2,32,128]{2,1,0:T(8,128)}, f32[2,1,32]{2,1,0:T(1,128)}) custom-call(s32[32,128]{1,0:T(8,128)} %bitcast.4, f32[4,128,128]{2,1,0:T(8,128)} %pot_hbm.1, bf16[256,384]{1,0:T(8,128)(2,1)} %constant.14.clone.first_hbm, bf16[256,384]{1,0:T(8,128)(2,1)} %constant.15.clone.up_a_hbm, bf16[2,64,256]{2,1,0:T(8,128)(2,1)} %constant.16.clone.up_b_hbm, ...), custom_call_target="tpu_custom_call" | custom-call | tf_op jit(solution)/shard_map/pallas_call | solution.py:460
  39.4 1.4 %copy.15 = f32[2,1,4096]{2,1,0:T(1,128)} copy(f32[2,1,4096]{2,1,0:T(1,128)} %bitcast.3) | data formatting | bytes 65536
  40.8 1.2 %copy.16 = f32[32,2,1]{0,2,1:T(1,128)} copy(f32[32,2,1]{0,2,1:T(1,128)} %bitcast.5) | data formatting | bytes 512
where the time goes:
time: 42.3 us; the launch traced here: 42 us
  Pallas kernels  38.8 us (92%)
  local copies, waits for them, and re-layouts  2.6 us (6%)
  between operations  0.64 us (2%)
    pallas_call x1, Pallas kernels, local(): pl.pallas_call(functools.partial(kernel, count, layers, extent, rows_msg,...  38.8 us
    unnamed x2, local copies, waits for them, and re-layouts  2.6 us

commit v1 on v0

--- a/solution.py
+++ b/solution.py
@@ -36,7 +36,7 @@
 
 
 @functools.lru_cache(None)
-def tables(extent, count, rows_msg, sub_rows):
+def tables(extent, count, rows_msg):
     half = extent // 2
     layers = extent // count
     cos, sin = phases(extent, half)
@@ -54,10 +54,6 @@
     up_b = np.concatenate([cos.T, sin.T], axis=1)
     down_b = np.block([[cos, -sin], [sin, cos]])
     down_a = np.concatenate([cos.T, sin.T], axis=0)
-    index = np.arange(count * sub_rows)
-    fold = np.zeros((2, count * sub_rows, LANES), np.float32)
-    fold[0, index, index % sub_rows] = 1.0
-    fold[1, index, sub_rows + index % sub_rows] = 1.0
     up_b_high, up_b_low = split_np(up_b)
     return (
         stack_np(first, 1),
@@ -66,7 +62,6 @@
         stack_np(down_b, 0),
         stack_np(down_a, 1),
         stack_np(last, 1),
-        fold.astype(ml_dtypes.bfloat16),
     )
 
 
@@ -88,14 +83,18 @@
     return jnp.where(values < extent // 2, values, values - extent)
 
 
+def bits_of(number, width):
+    return [lax.rem(lax.div(number, 2**k), 2) for k in range(width)]
+
+
 def kernel(
     count, layers, extent, rows_msg, group,
-    cells_hbm, pot_hbm, first_hbm, up_a_hbm, up_b_hbm, down_b_hbm, down_a_hbm, last_hbm, fold_hbm,
+    cells_hbm, pot_hbm, first_hbm, up_a_hbm, up_b_hbm, down_b_hbm, down_a_hbm, last_hbm,
     orb_hbm, applied_ref, sub_ref,
-    cells_ref, pot_ref, first_ref, up_a_ref, up_b_ref, down_b_ref, down_a_ref, last_ref, fold_ref,
-    orb, spread, place, cols, ids_out, ids_out2, ids_in, msg, arrived, pot_out, pot_in,
+    cells_ref, pot_ref, first_ref, up_a_ref, up_b_ref, down_b_ref, down_a_ref, last_ref,
+    orb, spread, place, ids_out, ids_in, msg, arrived, pot_out, pot_in,
     slab, pick_b, grid, freq, back, back_in, sums, sub_out, sub_in, kin, colrow, space,
-    win_sem, orb_sem, load_sem, send_sem, recv_sem, ids_sem, msg_sem,
+    win_sem, orb_sem, load_sem, send_sem, recv_sem, ids_sem, msg_sem, pot_sem,
 ):
     me = lax.axis_index("ga")
     half = extent // 2
@@ -104,31 +103,33 @@
     bands_all = orb.shape[1]
     sub_rows = bands_all // count
     parts = 2 * layers
-
+    width = count.bit_length() - 1
+    turns = [(1 - 2 * bit) * 2**k for k, bit in enumerate(bits_of(me, width))]
+
+    def peer(step):
+        return me + sum([turns[k] for k in range(width) if step >> k & 1], 0)
+
+    def turned(step, low):
+        wide = width - low
+        return me + sum([bit * turns[low + k] for k, bit in enumerate(bits_of(step, wide))], 0)
+
+    far_first = [peer(step) for step in range(count - 1, 0, -1)]
+    barrier = pltpu.get_barrier_semaphore()
+    load_cells = pltpu.make_async_copy(cells_hbm, cells_ref, load_sem.at[0])
+    load_cells.start()
     head = pltpu.make_async_copy(orb_hbm.at[:, 0:8, :], orb.at[:, 0:8, :], win_sem)
     head.start()
-    sources = (
-        cells_hbm, first_hbm, pot_hbm, up_a_hbm, up_b_hbm, down_b_hbm, down_a_hbm, last_hbm, fold_hbm
-    )
-    targets = (
-        cells_ref, first_ref, pot_ref, up_a_ref, up_b_ref, down_b_ref, down_a_ref, last_ref, fold_ref
-    )
+    for other in far_first:
+        pl.semaphore_signal(barrier, inc=1, device_id={"ga": other})
+    sources = (first_hbm, pot_hbm, up_a_hbm, up_b_hbm, down_b_hbm, down_a_hbm, last_hbm)
+    targets = (first_ref, pot_ref, up_a_ref, up_b_ref, down_b_ref, down_a_ref, last_ref)
     loads = [
-        pltpu.make_async_copy(source, target, load_sem.at[i])
+        pltpu.make_async_copy(source, target, load_sem.at[i + 1])
         for i, (source, target) in enumerate(zip(sources, targets))
     ]
-    load_cells, load_first, load_pot, load_up_a, load_up_b, load_down_b, load_down_a, load_last, load_fold = loads
+    load_first, load_pot, load_up_a, load_up_b, load_down_b, load_down_a, load_last = loads
     for load in loads:
         load.start()
-
-    barrier = pltpu.get_barrier_semaphore()
-
-    def greet(i, carry):
-        other = lax.rem(me + i, count)
-        pl.semaphore_signal(barrier, inc=1, device_id={"ga": other})
-        return carry
-
-    lax.fori_loop(1, count, greet, 0)
     rest = pltpu.make_async_copy(orb_hbm.at[:, 8:, :], orb.at[:, 8:, :], orb_sem)
     rest.start()
     groups = count // group
@@ -138,8 +139,7 @@
         own = pltpu.make_async_copy(source.at[me], target.at[me], landed)
         own.start()
 
-        def send(i, carry):
-            other = lax.rem(me + i, count)
+        for other in far_first:
             pltpu.make_async_remote_copy(
                 src_ref=source.at[other],
                 dst_ref=target.at[me],
@@ -147,9 +147,6 @@
                 recv_sem=landed,
                 device_id={"ga": other},
             ).start()
-            return carry
-
-        lax.fori_loop(1, count, send, 0)
 
     def arrive(target, phase):
         pltpu.make_async_copy(target, target, recv_sem.at[phase]).wait()
@@ -241,15 +238,17 @@
 
     load_pot.wait()
     for a in range(layers):
-        turned = jnp.transpose(pot_ref[a])
+        across = jnp.transpose(pot_ref[a])
         for d in range(count):
-            pot_out[d, a * layers : (a + 1) * layers, :] = turned[d * layers : (d + 1) * layers]
-    exchange(pot_out, pot_in, 2, recv_sem.at[2])
+            for l in range(layers):
+                pot_out[l, d, a : a + 1, :] = across[d * layers + l : d * layers + l + 1]
+    for l in range(layers):
+        exchange(pot_out.at[l], pot_in.at[l], 2, pot_sem.at[l])
 
     grid[...] = jnp.zeros_like(grid)
 
     def gather_group(step, carry):
-        g = lax.rem(my_group + step, groups)
+        g = lax.div(turned(step, group.bit_length() - 1), group)
         ids_view = ids_in.at[pl.ds(g * group, group)]
         pltpu.make_async_copy(ids_view, ids_view, ids_sem.at[g]).wait()
         msg_view = arrived.at[pl.ds(g * group, group)]
@@ -290,10 +289,9 @@
         space[0, l] = full[:extent, :extent] - full[extent:, extent:]
         space[1, l] = full[:extent, extent:] + full[extent:, :extent]
 
-    arrive(pot_in, 2)
     for l in range(layers):
-        planes = [pot_in[d, a * layers + l : a * layers + l + 1, :] for d in range(count) for a in range(layers)]
-        local_pot = jnp.concatenate(planes, axis=0)
+        pltpu.make_async_copy(pot_in.at[l], pot_in.at[l], pot_sem.at[l]).wait()
+        local_pot = pot_in[l].reshape(extent, extent)
         field = jnp.concatenate([space[0, l] * local_pot, space[1, l] * local_pot], axis=1)
         fallen = dot(stacked(field, 1), down_b_ref[...])
         product = dot(down_a_ref[...], stacked(fallen, 0))
@@ -322,9 +320,14 @@
         return jnp.concatenate(rows, axis=0)
 
     wide = 4
-
-    def give(index):
-        other = lax.rem(me + index, count)
+    rounds = count // wide
+
+    def who(i):
+        base = turned(rounds - 1 - i, 2) if width > 2 else me
+        near = [peer(step) - me for step in range(wide - 1, -1, -1)]
+        return [base + step for step in near]
+
+    def give(other):
         pltpu.make_async_remote_copy(
             src_ref=back.at[other],
             dst_ref=back_in.at[me],
@@ -336,21 +339,19 @@
     def take_some(i, carry):
         @pl.when(i > 0)
         def _():
-            for k in range(wide):
-                give((i - 1) * wide + k + 1)
-
-        who = [lax.rem(me + i * wide + k + 1, count) for k in range(wide)]
-        tiles = [take_columns(d) for d in who]
-        for d, tile in zip(who, tiles):
+            for other in who(i - 1):
+                give(other)
+
+        tiles = [take_columns(d) for d in who(i)]
+        for d, tile in zip(who(i), tiles):
             back[d] = tile
         return carry
 
-    lax.fori_loop(0, count // wide, take_some, 0)
-    for k in range(wide - 1):
-        give(count - wide + k + 1)
+    lax.fori_loop(0, rounds, take_some, 0)
+    for other in who(rounds - 1)[:-1]:
+        give(other)
     pltpu.make_async_copy(back.at[me], back_in.at[me], recv_sem.at[3]).start()
     load_last.wait()
-    load_fold.wait()
     arrive(back_in, 3)
 
     final = dot(last_ref[...], stacked(back_in[...].reshape(count * rows_msg, LANES), 0))
@@ -369,45 +370,78 @@
 
     rest.wait()
     tile_rows = 64
-
-    def rows_of(t, carry):
-        at = pl.ds(pl.multiple_of(t * tile_rows, tile_rows), tile_rows)
-        acc_re = jnp.zeros((tile_rows, LANES), F32)
-        acc_im = jnp.zeros((tile_rows, LANES), F32)
-        for r in range(blocks):
-            span = slice(r * LANES, (r + 1) * LANES)
-            a_re = applied_ref[0, r : r + 1, :]
-            a_im = applied_ref[1, r : r + 1, :]
-            o_re = orb[0, at, span]
-            o_im = orb[1, at, span]
-            acc_re = acc_re + (o_re * a_re + o_im * a_im)
-            acc_im = acc_im + (o_re * a_im - o_im * a_re)
-        sums[0, at, :] = acc_re
-        sums[1, at, :] = acc_im
+    owners = LANES // sub_rows
+    spans = count // owners
+    low = owners.bit_length() - 1
+    ones = jnp.ones((16, LANES), BF)
+
+    def tile_of(t):
+        return lax.div(turned(spans - 1 - t, low), owners) if spans > 1 else lax.div(me, owners)
+
+    def sweep(t, slot):
+        for piece in range(LANES // tile_rows):
+            start = tile_of(t) * LANES + piece * tile_rows
+            at = pl.ds(pl.multiple_of(start, tile_rows), tile_rows)
+            acc_re = jnp.zeros((tile_rows, LANES), F32)
+            acc_im = jnp.zeros((tile_rows, LANES), F32)
+            for r in range(blocks):
+                span = slice(r * LANES, (r + 1) * LANES)
+                a_re = applied_ref[0, r : r + 1, :]
+                a_im = applied_ref[1, r : r + 1, :]
+                o_re = orb[0, at, span]
+                o_im = orb[1, at, span]
+                acc_re = acc_re + (o_re * a_re + o_im * a_im)
+                acc_im = acc_im + (o_re * a_im - o_im * a_re)
+            rows = slice(piece * tile_rows, (piece + 1) * tile_rows)
+            sums[slot, 0, rows, :] = acc_re
+            sums[slot, 1, rows, :] = acc_im
+
+    def narrow(t, slot):
+        for part in range(2):
+            high, low_part = split(sums[slot, part])
+            line = dot(ones, high, NT) + dot(ones, low_part, NT)
+            sub_out[t, part : part + 1, :] = line[0:1] * (1.0 / (slots * count))
+
+    def share(t):
+        base = turned(spans - 1 - t, low) if spans > 1 else me
+        near = [peer(step) - me for step in range(owners - 1, -1, -1)]
+        return [base + step for step in near]
+
+    def publish(t, other):
+        pltpu.make_async_remote_copy(
+            src_ref=sub_out.at[t],
+            dst_ref=sub_in.at[me],
+            send_sem=send_sem.at[4],
+            recv_sem=recv_sem.at[4],
+            device_id={"ga": other},
+        ).start()
+
+    def sub_step(t, carry):
+        narrow(t - 1, lax.rem(t - 1, 2))
+        sweep(t, lax.rem(t, 2))
+        for other in share(t - 1):
+            publish(t - 1, other)
         return carry
 
-    lax.fori_loop(0, bands_all // tile_rows, rows_of, 0)
-    ones = jnp.ones((16, LANES), BF)
-    owner = lax.broadcasted_iota(jnp.int32, (count, bands_all), 1) // sub_rows
-    is_owner = owner == lax.broadcasted_iota(jnp.int32, (count, bands_all), 0)
-    folded = jnp.zeros((count, LANES), F32)
-    for part in range(2):
-        high, low = split(sums[part])
-        line = (dot(ones, high, NT) + dot(ones, low, NT))[0:1]
-        high, low = split(jnp.where(is_owner, line, 0.0))
-        folded = folded + dot(high, fold_ref[part]) + dot(low, fold_ref[part])
-    for d in range(count):
-        sub_out[d] = folded[d : d + 1] * (1.0 / (slots * count))
-    exchange(sub_out, sub_in, 4, recv_sem.at[4])
+    sweep(0, 0)
+    lax.fori_loop(1, spans, sub_step, 0)
+    narrow(spans - 1, (spans - 1) % 2)
+    for other in share(spans - 1)[:-1]:
+        publish(spans - 1, other)
+    pltpu.make_async_copy(sub_out.at[spans - 1], sub_in.at[me], recv_sem.at[4]).start()
     arrive(sub_in, 4)
     total = jnp.sum(sub_in[...], axis=0)
-    sub_ref[0] = total[:, :sub_rows]
-    sub_ref[1] = total[:, sub_rows : 2 * sub_rows]
+    padded = jnp.concatenate([total, jnp.zeros((6, LANES), F32)], axis=0)
+    offset = lax.rem(me, owners) * sub_rows
+    mine = pltpu.roll(padded, lax.rem(LANES - offset, LANES), 1)
+    sub_ref[...] = mine
     sent(ids_out, 0)
     sent(msg, 1)
-    sent(pot_out, 2)
+    for l in range(layers):
+        sent(pot_out.at[l], 2)
     sent(back, 3)
-    sent(sub_out, 4)
+    sub_view = sub_in.at[pl.ds(0, count - 1)]
+    pltpu.make_async_copy(sub_view, sub_view, send_sem.at[4]).wait()
 
 
 def local(orbitals, coeff_cells, potential):
@@ -421,7 +455,7 @@
     rows_msg = -(-parts // 8) * 8
     sub_rows = bands_all // count
     group = 8
-    constants = [jnp.asarray(t) for t in tables(extent, count, rows_msg, sub_rows)]
+    constants = [jnp.asarray(t) for t in tables(extent, count, rows_msg)]
     vmem = pl.BlockSpec(memory_space=pltpu.VMEM)
     staged = [(blocks, LANES), (layers, extent, extent)] + [t.shape for t in constants]
     kinds = [jnp.int32, F32] + [BF] * len(constants)
@@ -429,23 +463,21 @@
         pltpu.VMEM((2, bands_all, slots), F32),
         pltpu.VMEM((4 * half + 16, slots), BF),
         pltpu.VMEM((LANES, slots), BF),
-        pltpu.VMEM((8, LANES), F32),
         pltpu.VMEM((count, 1, LANES), F32),
-        pltpu.VMEM((8, LANES), F32),
         pltpu.VMEM((count, 1, LANES), F32),
         pltpu.VMEM((count, rows_msg, LANES), F32),
         pltpu.VMEM((count, rows_msg, LANES), F32),
-        pltpu.VMEM((count, layers * layers, LANES), F32),
-        pltpu.VMEM((count, layers * layers, LANES), F32),
+        pltpu.VMEM((layers, count, layers, LANES), F32),
+        pltpu.VMEM((layers, count, layers, LANES), F32),
         pltpu.VMEM((2 * parts * half, group * LANES), BF),
         pltpu.VMEM((half, group * LANES), BF),
         pltpu.VMEM((2 * parts * half, half), F32),
         pltpu.VMEM((layers * half, 4 * half), BF),
         pltpu.VMEM((count, rows_msg, LANES), F32),
         pltpu.VMEM((count, rows_msg, LANES), F32),
-        pltpu.VMEM((2, bands_all, LANES), F32),
-        pltpu.VMEM((count, 1, LANES), F32),
-        pltpu.VMEM((count, 1, LANES), F32),
+        pltpu.VMEM((2, 2, LANES, LANES), F32),
+        pltpu.VMEM((bands_all // LANES, 2, LANES), F32),
+        pltpu.VMEM((count, 2, LANES), F32),
         pltpu.VMEM((blocks, LANES), F32),
         pltpu.VMEM((4, blocks, LANES), jnp.int32),
         pltpu.VMEM((2, layers, extent, extent), F32),
@@ -456,12 +488,13 @@
         pltpu.SemaphoreType.DMA((5,)),
         pltpu.SemaphoreType.DMA((count // group,)),
         pltpu.SemaphoreType.DMA((count // group,)),
+        pltpu.SemaphoreType.DMA((layers,)),
     ]
     applied, sub = pl.pallas_call(
         functools.partial(kernel, count, layers, extent, rows_msg, group),
         out_shape=(
             jax.ShapeDtypeStruct((2, blocks, LANES), F32),
-            jax.ShapeDtypeStruct((2, 1, sub_rows), F32),
+            jax.ShapeDtypeStruct((8, LANES), F32),
         ),
         in_specs=[pl.BlockSpec(memory_space=pl.ANY)] * (3 + len(constants)),
         out_specs=(vmem, vmem),
@@ -471,7 +504,7 @@
         ),
     )(coeff_cells.reshape(blocks, LANES), potential, *constants, orbitals)
     applied = applied.reshape(2, 1, slots)
-    subspace = jnp.transpose(sub, (2, 0, 1))
+    subspace = jnp.transpose(sub[:2, :sub_rows])[:, :, None]
     return applied, subspace
 
 

time: 42.3 us -> 38.1 us (0.901)
  Pallas kernels: 38.8 us -> 34.6 us
    pallas_call x1, Pallas kernels: 38.8 us -> 34.6 us  [local(): pl.pallas_call(functools.partial(kernel, count, layers, extent, rows_msg,...]
    slice x0 -> x1, local copies, waits for them, and re-layouts: none -> 1.24 us  [local(): subspace = jnp.transpose(sub[:2, :sub_rows])[:, :, None]]
    unnamed x2 -> x1, local copies, waits for them, and re-layouts: 2.6 us -> 1.37 us
where the time goes in v1:
time: 38.1 us; the launch traced here: 37.8 us
  Pallas kernels  34.6 us (91%)
  local copies, waits for them, and re-layouts  2.62 us (7%)
  between operations  0.64 us (2%)
    pallas_call x1, Pallas kernels, local(): pl.pallas_call(functools.partial(kernel, count, layers, extent, rows_msg,...  34.6 us
    unnamed x1, local copies, waits for them, and re-layouts  1.37 us
    slice x1, local copies, waits for them, and re-layouts, local(): subspace = jnp.transpose(sub[:2, :sub_rows])[:, :, None]  1.24 us

profile of v1, /device:TPU:0, one launch (start us, length us, event | category | flops | bytes accessed | tf_op | source)
XLA Modules:
  0.0 37.8 jit_solution(15431442158396685714)
XLA Ops:
  0.6 34.6 %shard_map.104 = (f32[2,32,128]{2,1,0:T(8,128)}, f32[8,128]{1,0:T(8,128)}) custom-call(s32[32,128]{1,0:T(8,128)} %bitcast.8, f32[4,128,128]{2,1,0:T(8,128)} %pot_hbm.1, bf16[256,384]{1,0:T(8,128)(2,1)} %constant.12.clone.first_hbm, bf16[256,384]{1,0:T(8,128)(2,1)} %constant.13.clone.up_a_hbm, bf16[2,64,256]{2,1,0:T(8,128)(2,1)} %constant.14.clone.up_b_hbm, ...), custom_call_target="tpu_custom_call" | custom-call | tf_op jit(solution)/shard_map/pallas_call | solution.py:493
  35.2 1.2 %slice.3 = f32[2,32]{1,0:T(2,128)} slice(f32[8,128]{1,0:T(8,128)} %get-tuple-element.5), slice={[0:2], [0:32]} | slice | bytes 512 | tf_op jit(solution)/shard_map/slice | solution.py:507
  36.4 1.4 %copy.14 = f32[2,1,4096]{2,1,0:T(1,128)} copy(f32[2,1,4096]{2,1,0:T(1,128)} %bitcast.7) | data formatting | bytes 65536

commit v2 on v1

v2 whole, which is shorter than its diff:
```python
import functools

import jax
import jax.numpy as jnp
import ml_dtypes
import numpy as np
from jax import lax
from jax.experimental import pallas as pl
from jax.experimental.pallas import tpu as pltpu
from jax.sharding import PartitionSpec as P

RADIUS = 30
BF = jnp.bfloat16
F32 = jnp.float32
LANES = 128
FINE = 16
NN = (((1,), (0,)), ((), ()))
NT = (((1,), (1,)), ((), ()))


def split_np(table):
    high = table.astype(np.float32).astype(ml_dtypes.bfloat16)
    low = (table - high.astype(np.float64)).astype(np.float32).astype(ml_dtypes.bfloat16)
    return high, low


def stack_np(table, axis):
    high, low = split_np(table)
    return np.concatenate([high, high, low], axis=axis)


def phases(extent, half):
    index = np.arange(half)
    freq = np.where(index < half // 2, index, index - half)
    angle = 2.0 * np.pi * ((np.arange(extent)[:, None] * freq[None, :]) % extent) / extent
    return np.cos(angle), np.sin(angle)


@functools.lru_cache(None)
def tables(extent, count, rows_msg):
    half = extent // 2
    layers = extent // count
    cos, sin = phases(extent, half)
    first = np.zeros((count, rows_msg, 2 * half))
    last = np.zeros((2 * half, count, rows_msg))
    for l in range(layers):
        z = np.arange(count) * layers + l
        first[:, l, :half], first[:, l, half:] = cos[z], -sin[z]
        first[:, layers + l, :half], first[:, layers + l, half:] = sin[z], cos[z]
        last[:half, :, l], last[:half, :, layers + l] = cos[z].T, sin[z].T
        last[half:, :, l], last[half:, :, layers + l] = -sin[z].T, cos[z].T
    first = first.reshape(count * rows_msg, 2 * half)
    last = last.reshape(2 * half, count * rows_msg) / float(extent) ** 3
    up_a = np.block([[cos, -sin], [sin, cos]])
    up_b = np.concatenate([cos.T, sin.T], axis=1)
    down_b = np.block([[cos, -sin], [sin, cos]])
    down_a = np.concatenate([cos.T, sin.T], axis=0)
    up_b_high, up_b_low = split_np(up_b)
    return (
        stack_np(first, 1),
        stack_np(up_a, 1),
        np.concatenate([up_b_high, up_b_high, up_b_low, np.zeros_like(up_b_low)]),
        stack_np(down_b, 0),
        stack_np(down_a, 1),
        stack_np(last, 1),
    )


def dot(left, right, dims=NN):
    return lax.dot_general(left, right, dims, preferred_element_type=F32)


def split(values):
    high = values.astype(BF)
    return high, (values - high.astype(F32)).astype(BF)


def stacked(values, axis):
    high, low = split(values)
    return jnp.concatenate([high, low, high], axis=axis)


def signed(values, extent):
    return jnp.where(values < extent // 2, values, values - extent)


def rows_iota(rows):
    return lax.broadcasted_iota(jnp.int32, (rows, LANES), 0).astype(F32).astype(BF)


def tall(row, rows):
    block = jnp.broadcast_to(row, (16, LANES)).astype(BF)
    return jnp.concatenate([block] * (rows // 16), axis=0)


def matches(index, row):
    return jnp.where(index == tall(row, index.shape[0]), BF(1.0), BF(0.0))


def bits_of(number, width):
    return [lax.rem(lax.div(number, 2**k), 2) for k in range(width)]


def kernel(
    count, layers, extent, rows_msg, group,
    cells_hbm, pot_hbm, first_hbm, up_a_hbm, up_b_hbm, down_b_hbm, down_a_hbm, last_hbm,
    orb_hbm, applied_ref, sub_ref,
    cells_ref, pot_ref, first_ref, up_a_ref, up_b_ref, down_b_ref, down_a_ref, last_ref,
    orb, place, ids_out, ids_in, msg, arrived, pot_out, pot_in,
    pick, fines, grid, mesh, back, back_in, sums, sub_out, sub_in, added, mixed, kin, colrow, space,
    win_sem, orb_sem, load_sem, send_sem, recv_sem, ids_sem, msg_sem, pot_sem,
):
    me = lax.axis_index("ga")
    half = extent // 2
    slots = orb.shape[2]
    blocks = slots // LANES
    bands_all = orb.shape[1]
    sub_rows = bands_all // count
    parts = 2 * layers
    batch = min(2, layers)
    folds = half // FINE
    width = count.bit_length() - 1
    turns = [(1 - 2 * bit) * 2**k for k, bit in enumerate(bits_of(me, width))]

    def peer(step):
        return me + sum([turns[k] for k in range(width) if step >> k & 1], 0)

    def turned(step, low):
        wide = width - low
        return me + sum([bit * turns[low + k] for k, bit in enumerate(bits_of(step, wide))], 0)

    far_first = [peer(step) for step in range(count - 1, 0, -1)]
    barrier = pltpu.get_barrier_semaphore()
    load_cells = pltpu.make_async_copy(cells_hbm, cells_ref, load_sem.at[0])
    load_cells.start()
    head = pltpu.make_async_copy(orb_hbm.at[:, 0:8, :], orb.at[:, 0:8, :], win_sem)
    head.start()
    for other in far_first:
        pl.semaphore_signal(barrier, inc=1, device_id={"ga": other})
    sources = (first_hbm, pot_hbm, up_a_hbm, up_b_hbm, down_b_hbm, down_a_hbm, last_hbm)
    targets = (first_ref, pot_ref, up_a_ref, up_b_ref, down_b_ref, down_a_ref, last_ref)
    loads = [
        pltpu.make_async_copy(source, target, load_sem.at[i + 1])
        for i, (source, target) in enumerate(zip(sources, targets))
    ]
    load_first, load_pot, load_up_a, load_up_b, load_down_b, load_down_a, load_last = loads
    for load in loads:
        load.start()
    rest = pltpu.make_async_copy(orb_hbm.at[:, 8:, :], orb.at[:, 8:, :], orb_sem)
    rest.start()
    groups = count // group
    my_group = me // group

    def exchange(source, target, phase, landed):
        own = pltpu.make_async_copy(source.at[me], target.at[me], landed)
        own.start()

        for other in far_first:
            pltpu.make_async_remote_copy(
                src_ref=source.at[other],
                dst_ref=target.at[me],
                send_sem=send_sem.at[phase],
                recv_sem=landed,
                device_id={"ga": other},
            ).start()

    def arrive(target, phase):
        pltpu.make_async_copy(target, target, recv_sem.at[phase]).wait()

    def sent(source, phase):
        view = source.at[pl.ds(0, count - 1)]
        pltpu.make_async_copy(view, view, send_sem.at[phase]).wait()

    load_cells.wait()
    cells = cells_ref[...]
    live = cells >= 0
    column = jnp.right_shift(cells, extent.bit_length() - 1)
    rolled = pltpu.roll(column, 1, 1)
    lane = lax.broadcasted_iota(jnp.int32, cells.shape, 1)
    row = lax.broadcasted_iota(jnp.int32, cells.shape, 0)
    earlier = jnp.where(lane == 0, pltpu.roll(rolled, 1, 0), rolled)
    earlier = jnp.where((lane == 0) & (row == 0), -1, earlier)
    starts = live & (column != earlier)
    flags = starts.astype(F32).astype(BF)
    sq = lambda axis: lax.broadcasted_iota(jnp.int32, (LANES, LANES), axis)
    upper = (sq(0) <= sq(1)).astype(F32).astype(BF)
    inner = dot(flags, upper)
    totals = dot(flags, jnp.ones((LANES, LANES), BF))
    below = lax.broadcasted_iota(jnp.int32, (blocks, blocks), 1) < lax.broadcasted_iota(
        jnp.int32, (blocks, blocks), 0
    )
    outer = dot(below.astype(F32).astype(BF), totals.astype(BF))
    local = (inner + outer - 1.0).astype(jnp.int32)
    local = jnp.where(live, local, -1)
    safe = jnp.where(live, cells, 0)
    plane_c = safe % extent
    plane_b = safe // extent % extent
    plane_a = safe // (extent * extent)
    fa, fb, fc = signed(plane_a, extent), signed(plane_b, extent), signed(plane_c, extent)
    kinetic = (fa * fa + fb * fb + fc * fc).astype(F32) / (RADIUS * RADIUS)
    kin[...] = jnp.where(live, kinetic, 0.0)
    small_a = plane_a % half
    colrow[0] = local.astype(F32)
    colrow[1] = (plane_c % half).astype(F32)
    colrow[2] = jnp.where(starts, small_a % FINE, 0).astype(F32)
    colrow[3] = jnp.where(starts, small_a // FINE * half + plane_b % half, 0).astype(F32)

    head.wait()
    deep = rows_iota(half)
    full = rows_iota(LANES)
    sub_ids = lax.broadcasted_iota(jnp.int32, (16, LANES), 0)
    chunk = 4
    sticks = jnp.zeros((4 * half + 16, LANES), F32)
    for c in range(blocks // chunk):
        pieces = []
        for r in range(c * chunk, (c + 1) * chunk):
            span = slice(r * LANES, (r + 1) * LANES)
            at_depth = matches(deep, colrow[1, r : r + 1, :])
            lines = []
            for part in range(2):
                for value in split(orb[part, 0:1, span]):
                    lines.append(at_depth * tall(value.astype(F32), half))
            is_fine, is_wide = colrow[2, r : r + 1, :], colrow[3, r : r + 1, :]
            tail = jnp.where(sub_ids == 0, is_fine, jnp.where(sub_ids == 1, is_wide, 0.0))
            pieces.append(jnp.concatenate(lines + [tail.astype(BF)], axis=0))
            place[:, span] = matches(full, colrow[0, r : r + 1, :])
        span = slice(c * chunk * LANES, (c + 1) * chunk * LANES)
        sticks = sticks + dot(jnp.concatenate(pieces, axis=1), place[:, span], NT)
    code = sticks[4 * half : 4 * half + 1] * (folds * half) + sticks[4 * half + 1 : 4 * half + 2]

    def copy_ids(d, carry):
        ids_out[d] = code
        return carry

    lax.fori_loop(0, count, copy_ids, 0)
    both = jnp.concatenate(
        [
            sticks[0:half] + sticks[half : 2 * half],
            sticks[2 * half : 3 * half] + sticks[3 * half : 4 * half],
        ],
        axis=0,
    )
    load_first.wait()
    msg[...] = dot(first_ref[...], stacked(both, 0)).reshape(count, rows_msg, LANES)
    pl.semaphore_wait(barrier, count - 1)
    exchange(ids_out, ids_in, 0, ids_sem.at[my_group])
    exchange(msg, arrived, 1, msg_sem.at[my_group])

    load_pot.wait()
    for a in range(layers):
        across = jnp.transpose(pot_ref[a])
        for d in range(count):
            for l in range(layers):
                row = l % batch * layers + a
                pot_out[l // batch, d, row : row + 1, :] = across[d * layers + l : d * layers + l + 1]
    for c in range(layers // batch):
        exchange(pot_out.at[c], pot_in.at[c], 2, pot_sem.at[c])

    grid[...] = jnp.zeros_like(grid)
    broad = rows_iota(folds * half)

    def gather_group(step, carry):
        g = lax.div(turned(step, group.bit_length() - 1), group)
        ids_view = ids_in.at[pl.ds(g * group, group)]
        pltpu.make_async_copy(ids_view, ids_view, ids_sem.at[g]).wait()
        msg_view = arrived.at[pl.ds(g * group, group)]
        pltpu.make_async_copy(msg_view, msg_view, msg_sem.at[g]).wait()
        pieces = []
        for k in range(group):
            d = g * group + k
            code = ids_in[d]
            is_fine = jnp.floor(code * (1.0 / (folds * half)))
            fines[d] = is_fine
            span = pl.ds(pl.multiple_of(d * LANES, LANES), LANES)
            pick[:, span] = matches(broad, code - is_fine * (folds * half))
            high, low = split(arrived[d])
            high, low = high.astype(F32), low.astype(F32)
            here = jnp.broadcast_to(is_fine, (rows_msg, LANES))
            lines = [jnp.where(here == f, high, 0.0) for f in range(FINE)]
            lines += [jnp.where(here == f, low, 0.0) for f in range(FINE)]
            pieces.append(jnp.concatenate(lines, axis=0).astype(BF))
        span = pl.ds(pl.multiple_of(g * group * LANES, group * LANES), group * LANES)
        grid[...] += dot(jnp.concatenate(pieces, axis=1), pick[:, span], NT)
        return carry

    lax.fori_loop(0, groups, gather_group, 0)
    load_up_a.wait()
    load_up_b.wait()
    load_down_b.wait()
    load_down_a.wait()

    rows_mesh = FINE * rows_msg
    halves = folds * half // LANES
    per = LANES // half
    both = grid[0:rows_mesh] + grid[rows_mesh:]
    for h in range(halves):
        mesh[h] = both[:, h * LANES : (h + 1) * LANES]

    lines = []
    for part in range(2):
        for h in range(halves):
            blocks_of = [
                mesh[h, pl.ds(part * layers + l, FINE, stride=rows_msg), :] for l in range(layers)
            ]
            for q in range(per):
                lines.append(
                    jnp.concatenate([block[:, q * half : (q + 1) * half] for block in blocks_of], axis=1)
                )
    lifted = dot(up_a_ref[...], stacked(jnp.concatenate(lines, axis=0), 0))
    for l in range(layers):
        plane = lifted[:, l * half : (l + 1) * half]
        high = plane.astype(BF).astype(F32)
        pair = jnp.concatenate([high, plane - high], axis=1).astype(BF)
        whole = dot(jnp.concatenate([pair, pair], axis=1), up_b_ref[...])
        space[0, l] = whole[:extent, :extent] - whole[extent:, extent:]
        space[1, l] = whole[:extent, extent:] + whole[extent:, :extent]

    mesh[...] = jnp.zeros_like(mesh)
    lane_half = lax.broadcasted_iota(jnp.int32, (half, 2 * half), 1)
    for c in range(layers // batch):
        pltpu.make_async_copy(pot_in.at[c], pot_in.at[c], pot_sem.at[c]).wait()
        fallen = []
        for i in range(batch):
            l = c * batch + i
            local_pot = pot_in[c, :, i * layers : (i + 1) * layers, :].reshape(extent, extent)
            field = jnp.concatenate([space[0, l] * local_pot, space[1, l] * local_pot], axis=1)
            fallen.append(dot(stacked(field, 1), down_b_ref[...]))
        products = dot(down_a_ref[...], stacked(jnp.concatenate(fallen, axis=1), 0))
        for i in range(batch):
            product = products[:, i * 2 * half : (i + 1) * 2 * half]
            swap = pltpu.roll(product[half:], half, 1)
            total = product[:half] + jnp.where(lane_half < half, swap, -swap)
            for part in range(2):
                block = total[:, part * half : (part + 1) * half]
                for h in range(halves):
                    sides = [block[q * FINE : (q + 1) * FINE] for q in range(h * per, (h + 1) * per)]
                    line = jnp.concatenate(sides, axis=1)
                    at = part * layers + c * batch + i
                    mesh[h, pl.ds(at, FINE, stride=rows_msg), :] = line

    wide = 4
    rounds = count // wide
    left = jnp.concatenate(split(jnp.concatenate([mesh[h] for h in range(halves)], axis=1)), axis=0)

    def give(other):
        pltpu.make_async_remote_copy(
            src_ref=back.at[other],
            dst_ref=back_in.at[me],
            send_sem=send_sem.at[3],
            recv_sem=recv_sem.at[3],
            device_id={"ga": other},
        ).start()

    def first_of(i):
        return lax.div(peer((rounds - 1 - i) * wide), wide) * wide

    def find(i):
        span = pl.ds(pl.multiple_of(first_of(i) * LANES, wide * LANES), wide * LANES)
        return dot(left, pick[:, span])

    found = find(0)
    for i in range(rounds):
        following = find(i + 1) if i + 1 < rounds else None
        for k in range(wide):
            here = jnp.broadcast_to(fines[first_of(i) + k], (rows_msg, LANES))
            tile = jnp.zeros((rows_msg, LANES), F32)
            for f in range(FINE):
                cut = (slice(f * rows_msg, (f + 1) * rows_msg), slice(k * LANES, (k + 1) * LANES))
                tile = tile + jnp.where(here == f, found[:rows_mesh][cut] + found[rows_mesh:][cut], 0.0)
            back[first_of(i) + k] = tile
        if i > 0:
            for step in range(wide):
                give(peer((rounds - i) * wide + wide - 1 - step))
        found = following
    for step in range(wide - 1):
        give(peer(wide - 1 - step))
    pltpu.make_async_copy(back.at[me], back_in.at[me], recv_sem.at[3]).start()
    rest.wait()

    def add(t, carry):
        at = pl.ds(pl.multiple_of(t * 16, 16), 16)
        added[at, :] = orb[0, at, :] + orb[1, at, :]
        return carry

    lax.fori_loop(0, bands_all // 16, add, 0)
    load_last.wait()
    arrive(back_in, 3)

    sub_half = lax.broadcasted_iota(jnp.int32, (half, LANES), 0).astype(F32)
    final = dot(last_ref[...], stacked(back_in[...].reshape(count * rows_msg, LANES), 0))
    high, low = split(final)
    final_cat = jnp.concatenate([high, low], axis=1)
    place_rows = jnp.concatenate([place[...], place[...]], axis=0)
    spread_back = dot(final_cat, place_rows)
    for r in range(blocks):
        at_depth = sub_half == colrow[1, r : r + 1, :]
        span = slice(r * LANES, (r + 1) * LANES)
        k_row = kin[r : r + 1, :]
        for part in range(2):
            block = spread_back[part * half : (part + 1) * half, span]
            value = jnp.sum(jnp.where(at_depth, block, 0.0), axis=0, keepdims=True)
            applied_ref[part, r : r + 1, :] = value + k_row * orb[part, 0:1, span]

    u, v = applied_ref[0], applied_ref[1]
    mixed[0], mixed[1], mixed[2] = u, u - v, u + v
    tile_rows = 64
    owners = tile_rows // sub_rows
    spans = count // owners
    low = owners.bit_length() - 1

    def tile_of(t):
        return lax.div(turned(spans - 1 - t, low), owners) if spans > 1 else lax.div(me, owners)

    def sweep(t, slot):
        at = pl.ds(pl.multiple_of(tile_of(t) * tile_rows, tile_rows), tile_rows)
        acc = [jnp.zeros((tile_rows, LANES), F32) for _ in range(3)]
        for r in range(blocks):
            span = slice(r * LANES, (r + 1) * LANES)
            acc[0] = acc[0] + added[at, span] * mixed[0, r : r + 1, :]
            acc[1] = acc[1] + orb[1, at, span] * mixed[1, r : r + 1, :]
            acc[2] = acc[2] + orb[0, at, span] * mixed[2, r : r + 1, :]
        sums[slot, 0] = acc[0] - acc[1]
        sums[slot, 1] = acc[2] - acc[0]

    def narrow(t, slot):
        both = sums[slot].reshape(2 * tile_rows, LANES)
        line = jnp.sum(jnp.transpose(both), axis=0, keepdims=True)
        sub_out[t] = line * (1.0 / (slots * count))

    def share(t):
        base = turned(spans - 1 - t, low) if spans > 1 else me
        near = [peer(step) - me for step in range(owners - 1, -1, -1)]
        return [base + step for step in near]

    def publish(t, other):
        pltpu.make_async_remote_copy(
            src_ref=sub_out.at[t],
            dst_ref=sub_in.at[me],
            send_sem=send_sem.at[4],
            recv_sem=recv_sem.at[4],
            device_id={"ga": other},
        ).start()

    def sub_step(t, carry):
        narrow(t - 1, lax.rem(t - 1, 2))
        sweep(t, lax.rem(t, 2))
        for other in share(t - 1):
            publish(t - 1, other)
        return carry

    sweep(0, 0)
    lax.fori_loop(1, spans, sub_step, 0)
    narrow(spans - 1, (spans - 1) % 2)
    for other in share(spans - 1)[:-1]:
        publish(spans - 1, other)
    pltpu.make_async_copy(sub_out.at[spans - 1], sub_in.at[me], recv_sem.at[4]).start()
    arrive(sub_in, 4)
    total = jnp.broadcast_to(jnp.sum(sub_in[...], axis=0), (8, LANES))
    offset = lax.rem(me, owners) * sub_rows
    mine = pltpu.roll(total, lax.rem(LANES - offset, LANES), 1)
    sub_ref[0] = mine[0:1, :sub_rows]
    sub_ref[1] = mine[0:1, tile_rows : tile_rows + sub_rows]
    sent(ids_out, 0)
    sent(msg, 1)
    for c in range(layers // batch):
        sent(pot_out.at[c], 2)
    sent(back, 3)
    sub_view = sub_in.at[pl.ds(0, count - 1)]
    pltpu.make_async_copy(sub_view, sub_view, send_sem.at[4]).wait()


def emit(applied_ref, sub_ref, applied_out, sub_out):
    applied_out[...] = applied_ref[...]
    sub_out[...] = sub_ref[...]


def local(orbitals, coeff_cells, potential):
    count = lax.axis_size("ga")
    extent = potential.shape[1]
    layers = extent // count
    half = extent // 2
    bands_all, slots = orbitals.shape[1], orbitals.shape[2]
    blocks = slots // LANES
    parts = 2 * layers
    rows_msg = -(-parts // 8) * 8
    sub_rows = bands_all // count
    group = 8
    batch = min(2, layers)
    folds = half // FINE
    constants = [jnp.asarray(t) for t in tables(extent, count, rows_msg)]
    vmem = pl.BlockSpec(memory_space=pltpu.VMEM)
    staged = [(blocks, LANES), (layers, extent, extent)] + [t.shape for t in constants]
    kinds = [jnp.int32, F32] + [BF] * len(constants)
    scratch = [pltpu.VMEM(shape, kind) for shape, kind in zip(staged, kinds)] + [
        pltpu.VMEM((2, bands_all, slots), F32),
        pltpu.VMEM((LANES, slots), BF),
        pltpu.VMEM((count, 1, LANES), F32),
        pltpu.VMEM((count, 1, LANES), F32),
        pltpu.VMEM((count, rows_msg, LANES), F32),
        pltpu.VMEM((count, rows_msg, LANES), F32),
        pltpu.VMEM((layers // batch, count, batch * layers, LANES), F32),
        pltpu.VMEM((layers // batch, count, batch * layers, LANES), F32),
        pltpu.VMEM((folds * half, count * LANES), BF),
        pltpu.VMEM((count, 1, LANES), F32),
        pltpu.VMEM((2 * FINE * rows_msg, folds * half), F32),
        pltpu.VMEM((folds * half // LANES, FINE * rows_msg, LANES), F32),
        pltpu.VMEM((count, rows_msg, LANES), F32),
        pltpu.VMEM((count, rows_msg, LANES), F32),
        pltpu.VMEM((2, 2, 64, LANES), F32),
        pltpu.VMEM((bands_all // 64, 1, LANES), F32),
        pltpu.VMEM((count, 1, LANES), F32),
        pltpu.VMEM((bands_all, slots), F32),
        pltpu.VMEM((3, blocks, LANES), F32),
        pltpu.VMEM((blocks, LANES), F32),
        pltpu.VMEM((4, blocks, LANES), F32),
        pltpu.VMEM((2, layers, extent, extent), F32),
        pltpu.SemaphoreType.DMA,
        pltpu.SemaphoreType.DMA,
        pltpu.SemaphoreType.DMA((len(staged),)),
        pltpu.SemaphoreType.DMA((5,)),
        pltpu.SemaphoreType.DMA((5,)),
        pltpu.SemaphoreType.DMA((count // group,)),
        pltpu.SemaphoreType.DMA((count // group,)),
        pltpu.SemaphoreType.DMA((layers // batch,)),
    ]
    applied, sub = pl.pallas_call(
        functools.partial(kernel, count, layers, extent, rows_msg, group),
        out_shape=(
            pltpu.VMEM((2, blocks, LANES), F32),
            pltpu.VMEM((2, 1, sub_rows), F32),
        ),
        in_specs=[pl.BlockSpec(memory_space=pl.ANY)] * (3 + len(constants)),
        out_specs=(vmem, vmem),
        scratch_shapes=scratch,
        compiler_params=pltpu.CompilerParams(
            collective_id=0, has_side_effects=True, vmem_limit_bytes=60 * 1024 * 1024
        ),
    )(coeff_cells.reshape(blocks, LANES), potential, *constants, orbitals)
    applied, sub = pl.pallas_call(
        emit,
        out_shape=(
            jax.ShapeDtypeStruct(applied.shape, F32),
            jax.ShapeDtypeStruct(sub.shape, F32),
        ),
        in_specs=[vmem, vmem],
        out_specs=(vmem, vmem),
        compiler_params=pltpu.CompilerParams(vmem_limit_bytes=1024 * 1024),
    )(applied, sub)
    applied = applied.reshape(2, 1, slots)
    subspace = jnp.transpose(sub, (2, 0, 1))
    return applied, subspace


def solution(mesh):
    in_specs = (P(None, "kpt", "ga"), P("ga"), P("ga", None, None))
    out_specs = (P(None, "kpt", "ga"), P("ga", None, "kpt"))
    return jax.shard_map(local, mesh=mesh, in_specs=in_specs, out_specs=out_specs, check_vma=False)
```

time: 38.1 us -> 33.1 us (0.87)
  local copies, waits for them, and re-layouts: 2.62 us -> 0 us
  Pallas kernels: 34.6 us -> 32.2 us
    pallas_call x1, Pallas kernels: 34.6 us -> 31.6 us  [local(): pl.pallas_call(functools.partial(kernel, count, layers, extent, rows_msg,...]
    unnamed x1 -> x0, local copies, waits for them, and re-layouts: 1.37 us -> none
    slice x1 -> x0, local copies, waits for them, and re-layouts: 1.24 us -> none  [local(): subspace = jnp.transpose(sub[:2, :sub_rows])[:, :, None]]
    pallas_call x0 -> x1, Pallas kernels: none -> 0.62 us  [local(): pl.pallas_call(emit, out_shape=(jax.ShapeDtypeStruct(applied.shape, F32),...]
where the time goes in v2:
time: 33.1 us; the launch traced here: 32.9 us
  Pallas kernels  32.2 us (97%)
  between operations  0.64 us (2%)
    pallas_call x1, Pallas kernels, local(): pl.pallas_call(functools.partial(kernel, count, layers, extent, rows_msg,...  31.6 us

profile of v2, /device:TPU:0, one launch (start us, length us, event | category | flops | bytes accessed | tf_op | source)
XLA Modules:
  0.0 32.9 jit_solution(6290220766630128576)
XLA Ops:
  0.6 31.6 %shard_map.104 = (f32[2,32,128]{2,1,0:T(8,128)S(1)}, f32[2,1,32]{2,1,0:T(1,128)S(1)}) custom-call(s32[32,128]{1,0:T(8,128)} %bitcast.3, f32[4,128,128]{2,1,0:T(8,128)} %pot_hbm.1, bf16[256,384]{1,0:T(8,128)(2,1)} %constant.12.clone.first_hbm, bf16[256,384]{1,0:T(8,128)(2,1)} %constant.13.clone.up_a_hbm, bf16[256,256]{1,0:T(8,128)(2,1)} %constant.14.clone.up_b_hbm, ...), custom_call_target="tpu_custom_call" | custom-call | tf_op jit(solution)/shard_map/pallas_call | solution.py:526
  32.2 0.6 %shard_map.105 = (f32[2,32,128]{2,1,0:T(8,128)}, f32[2,1,32]{2,1,0:T(1,128)}) custom-call(f32[2,32,128]{2,1,0:T(8,128)S(1)} %get-tuple-element.6.applied_ref, f32[2,1,32]{2,1,0:T(1,128)S(1)} %get-tuple-element.7.sub_ref), custom_call_target="tpu_custom_call" | custom-call | tf_op jit(solution)/shard_map/pallas_call | solution.py:539

commit v3 on v2

--- a/solution.py
+++ b/solution.py
@@ -66,6 +66,22 @@
     )
 
 
+def sheared(values, shifts):
+    row = lax.broadcasted_iota(jnp.int32, values.shape, 0) % 4
+    turned = [pltpu.roll(values, shift, 1) for shift in shifts]
+    return jnp.where(row == 0, turned[0], jnp.where(row == 1, turned[1], turned[2]))
+
+
+def most_columns(extent, count):
+    index = np.arange(extent)
+    square = np.where(index < extent // 2, index, index - extent) ** 2
+    return -(-int((square[:, None] + square[None, :] <= RADIUS * RADIUS).sum()) // count)
+
+
+def is_narrow(extent, count, parts):
+    return parts == 8 and most_columns(extent, count) <= 3 * (LANES // 4)
+
+
 def dot(left, right, dims=NN):
     return lax.dot_general(left, right, dims, preferred_element_type=F32)
 
@@ -119,6 +135,8 @@
     parts = 2 * layers
     batch = min(2, layers)
     folds = half // FINE
+    narrow_msg = is_narrow(extent, count, parts)
+    room = 3 * (LANES // 4)
     width = count.bit_length() - 1
     turns = [(1 - 2 * bit) * 2**k for k, bit in enumerate(bits_of(me, width))]
 
@@ -228,11 +246,6 @@
         sticks = sticks + dot(jnp.concatenate(pieces, axis=1), place[:, span], NT)
     code = sticks[4 * half : 4 * half + 1] * (folds * half) + sticks[4 * half + 1 : 4 * half + 2]
 
-    def copy_ids(d, carry):
-        ids_out[d] = code
-        return carry
-
-    lax.fori_loop(0, count, copy_ids, 0)
     both = jnp.concatenate(
         [
             sticks[0:half] + sticks[half : 2 * half],
@@ -241,9 +254,21 @@
         axis=0,
     )
     load_first.wait()
-    msg[...] = dot(first_ref[...], stacked(both, 0)).reshape(count, rows_msg, LANES)
+    sheet = dot(first_ref[...], stacked(both, 0)).reshape(count, rows_msg, LANES)
+    if narrow_msg:
+        row_of = lax.broadcasted_iota(jnp.int32, (count, rows_msg, LANES), 1)
+        lane_of = lax.broadcasted_iota(jnp.int32, (count, rows_msg, LANES), 2)
+        ends = jnp.where(row_of < 4, sheet[:, rows_msg - 1 : rows_msg, :], code[None])
+        ends = ends.reshape(count * rows_msg, LANES)
+        ends = sheared(ends, [room, room - LANES // 4, room - LANES // 2])
+        sheet = jnp.where(lane_of < room, sheet, ends.reshape(count, rows_msg, LANES))
+        msg[...] = sheet[:, : rows_msg - 1, :]
+    else:
+        msg[...] = sheet
+        ids_out[...] = jnp.broadcast_to(code[None], ids_out.shape)
     pl.semaphore_wait(barrier, count - 1)
-    exchange(ids_out, ids_in, 0, ids_sem.at[my_group])
+    if not narrow_msg:
+        exchange(ids_out, ids_in, 0, ids_sem.at[my_group])
     exchange(msg, arrived, 1, msg_sem.at[my_group])
 
     load_pot.wait()
@@ -258,22 +283,36 @@
 
     grid[...] = jnp.zeros_like(grid)
     broad = rows_iota(folds * half)
+    row_of = lax.broadcasted_iota(jnp.int32, (rows_msg, LANES), 0)
+    lane_of = lax.broadcasted_iota(jnp.int32, (rows_msg, LANES), 1)
 
     def gather_group(step, carry):
         g = lax.div(turned(step, group.bit_length() - 1), group)
-        ids_view = ids_in.at[pl.ds(g * group, group)]
-        pltpu.make_async_copy(ids_view, ids_view, ids_sem.at[g]).wait()
+        if not narrow_msg:
+            ids_view = ids_in.at[pl.ds(g * group, group)]
+            pltpu.make_async_copy(ids_view, ids_view, ids_sem.at[g]).wait()
         msg_view = arrived.at[pl.ds(g * group, group)]
         pltpu.make_async_copy(msg_view, msg_view, msg_sem.at[g]).wait()
         pieces = []
         for k in range(group):
             d = g * group + k
-            code = ids_in[d]
+            tile = arrived[d]
+            if narrow_msg:
+                tile = jnp.concatenate([tile, tile[0:1]], axis=0)
+                ends = sheared(tile, [LANES // 4, LANES // 2, room])
+                ends = jnp.where(lane_of // (LANES // 4) == row_of % 4, ends, 0.0)
+                ends = jnp.where(row_of % 4 < 3, ends, 0.0)
+                final_row = ends[0:1] + ends[1:2] + ends[2:3]
+                code = ends[4:5] + ends[5:6] + ends[6:7]
+                tile = jnp.where(row_of == rows_msg - 1, final_row, tile)
+                tile = jnp.where(lane_of < room, tile, 0.0)
+            else:
+                code = ids_in[d]
             is_fine = jnp.floor(code * (1.0 / (folds * half)))
             fines[d] = is_fine
             span = pl.ds(pl.multiple_of(d * LANES, LANES), LANES)
             pick[:, span] = matches(broad, code - is_fine * (folds * half))
-            high, low = split(arrived[d])
+            high, low = split(tile)
             high, low = high.astype(F32), low.astype(F32)
             here = jnp.broadcast_to(is_fine, (rows_msg, LANES))
             lines = [jnp.where(here == f, high, 0.0) for f in range(FINE)]
@@ -460,7 +499,8 @@
     mine = pltpu.roll(total, lax.rem(LANES - offset, LANES), 1)
     sub_ref[0] = mine[0:1, :sub_rows]
     sub_ref[1] = mine[0:1, tile_rows : tile_rows + sub_rows]
-    sent(ids_out, 0)
+    if not narrow_msg:
+        sent(ids_out, 0)
     sent(msg, 1)
     for c in range(layers // batch):
         sent(pot_out.at[c], 2)
@@ -485,6 +525,7 @@
     rows_msg = -(-parts // 8) * 8
     sub_rows = bands_all // count
     group = 8
+    narrow = int(is_narrow(extent, count, parts))
     batch = min(2, layers)
     folds = half // FINE
     constants = [jnp.asarray(t) for t in tables(extent, count, rows_msg)]
@@ -496,8 +537,8 @@
         pltpu.VMEM((LANES, slots), BF),
         pltpu.VMEM((count, 1, LANES), F32),
         pltpu.VMEM((count, 1, LANES), F32),
-        pltpu.VMEM((count, rows_msg, LANES), F32),
-        pltpu.VMEM((count, rows_msg, LANES), F32),
+        pltpu.VMEM((count, rows_msg - narrow, LANES), F32),
+        pltpu.VMEM((count, rows_msg - narrow, LANES), F32),
         pltpu.VMEM((layers // batch, count, batch * layers, LANES), F32),
         pltpu.VMEM((layers // batch, count, batch * layers, LANES), F32),
         pltpu.VMEM((folds * half, count * LANES), BF),

time: 33.1 us -> 32.4 us (0.979)
  Pallas kernels: 32.2 us -> 31.5 us
    pallas_call x1, Pallas kernels: 31.6 us -> 30.9 us  [local(): pl.pallas_call(functools.partial(kernel, count, layers, extent, rows_msg,...]
where the time goes in v3:
time: 32.4 us; the launch traced here: 32.2 us
  Pallas kernels  31.5 us (97%)
  between operations  0.64 us (2%)
    pallas_call x1, Pallas kernels, local(): pl.pallas_call(functools.partial(kernel, count, layers, extent, rows_msg,...  30.9 us

profile of v3, /device:TPU:0, one launch (start us, length us, event | category | flops | bytes accessed | tf_op | source)
XLA Modules:
  0.0 32.2 jit_solution(4442026674956609414)
XLA Ops:
  0.6 30.9 %shard_map.104 = (f32[2,32,128]{2,1,0:T(8,128)S(1)}, f32[2,1,32]{2,1,0:T(1,128)S(1)}) custom-call(s32[32,128]{1,0:T(8,128)} %bitcast.3, f32[4,128,128]{2,1,0:T(8,128)} %pot_hbm.1, bf16[256,384]{1,0:T(8,128)(2,1)} %constant.12.clone.first_hbm, bf16[256,384]{1,0:T(8,128)(2,1)} %constant.13.clone.up_a_hbm, bf16[256,256]{1,0:T(8,128)(2,1)} %constant.14.clone.up_b_hbm, ...), custom_call_target="tpu_custom_call" | custom-call | tf_op jit(solution)/shard_map/pallas_call | solution.py:567
  31.5 0.6 %shard_map.105 = (f32[2,32,128]{2,1,0:T(8,128)}, f32[2,1,32]{2,1,0:T(1,128)}) custom-call(f32[2,32,128]{2,1,0:T(8,128)S(1)} %get-tuple-element.6.applied_ref, f32[2,1,32]{2,1,0:T(1,128)S(1)} %get-tuple-element.7.sub_ref), custom_call_target="tpu_custom_call" | custom-call | tf_op jit(solution)/shard_map/pallas_call | solution.py:580

commit v4 on v3

--- a/solution.py
+++ b/solution.py
@@ -37,7 +37,7 @@
 
 
 @functools.lru_cache(None)
-def tables(extent, count, rows_msg):
+def tables(extent, count, rows_msg, batch):
     half = extent // 2
     layers = extent // count
     cos, sin = phases(extent, half)
@@ -50,7 +50,14 @@
         last[:half, :, l], last[:half, :, layers + l] = cos[z].T, sin[z].T
         last[half:, :, l], last[half:, :, layers + l] = -sin[z].T, cos[z].T
     first = first.reshape(count * rows_msg, 2 * half)
-    last = last.reshape(2 * half, count * rows_msg) / float(extent) ** 3
+    order = [
+        part * layers + c * batch + i
+        for c in range(layers // batch)
+        for part in range(2)
+        for i in range(batch)
+    ]
+    last = last[:, :, order].reshape(2 * half, count, layers // batch, 2 * batch)
+    last = last.transpose(0, 2, 1, 3).reshape(2 * half, 2 * layers * count) / float(extent) ** 3
     up_a = np.block([[cos, -sin], [sin, cos]])
     up_b = np.concatenate([cos.T, sin.T], axis=1)
     down_b = np.block([[cos, -sin], [sin, cos]])
@@ -123,8 +130,8 @@
     orb_hbm, applied_ref, sub_ref,
     cells_ref, pot_ref, first_ref, up_a_ref, up_b_ref, down_b_ref, down_a_ref, last_ref,
     orb, place, ids_out, ids_in, msg, arrived, pot_out, pot_in,
-    pick, fines, grid, mesh, back, back_in, sums, sub_out, sub_in, added, mixed, kin, colrow, space,
-    win_sem, orb_sem, load_sem, send_sem, recv_sem, ids_sem, msg_sem, pot_sem,
+    pick, fines, grid, mesh, freq, back, back_in, sums, sub_out, sub_in, added, mixed, kin, colrow, space,
+    win_sem, orb_sem, load_sem, send_sem, recv_sem, ids_sem, msg_sem, pot_sem, back_sem,
 ):
     me = lax.axis_index("ga")
     half = extent // 2
@@ -266,11 +273,6 @@
     else:
         msg[...] = sheet
         ids_out[...] = jnp.broadcast_to(code[None], ids_out.shape)
-    pl.semaphore_wait(barrier, count - 1)
-    if not narrow_msg:
-        exchange(ids_out, ids_in, 0, ids_sem.at[my_group])
-    exchange(msg, arrived, 1, msg_sem.at[my_group])
-
     load_pot.wait()
     for a in range(layers):
         across = jnp.transpose(pot_ref[a])
@@ -278,6 +280,11 @@
             for l in range(layers):
                 row = l % batch * layers + a
                 pot_out[l // batch, d, row : row + 1, :] = across[d * layers + l : d * layers + l + 1]
+    pl.semaphore_wait(barrier, count - 1)
+    if not narrow_msg:
+        exchange(ids_out, ids_in, 0, ids_sem.at[my_group])
+    exchange(msg, arrived, 1, msg_sem.at[my_group])
+
     for c in range(layers // batch):
         exchange(pot_out.at[c], pot_in.at[c], 2, pot_sem.at[c])
 
@@ -354,7 +361,56 @@
         space[0, l] = whole[:extent, :extent] - whole[extent:, extent:]
         space[1, l] = whole[:extent, extent:] + whole[extent:, :extent]
 
-    mesh[...] = jnp.zeros_like(mesh)
+    rows_back = 2 * batch
+    share_of = 8 // rows_back
+    wide = 8
+    rounds = count // wide
+    sub_of = (lax.broadcasted_iota(jnp.int32, (8, LANES), 0) // rows_back).astype(F32)
+
+    def first_of(i):
+        return lax.div(peer((rounds - 1 - i) * wide), wide) * wide
+
+    def give(c, other):
+        pltpu.make_async_remote_copy(
+            src_ref=back.at[c, other],
+            dst_ref=back_in.at[c, me],
+            send_sem=send_sem.at[3],
+            recv_sem=back_sem.at[c],
+            device_id={"ga": other},
+        ).start()
+
+    def take(c):
+        sheet = jnp.concatenate([freq[c, h] for h in range(halves)], axis=1)
+        left = jnp.concatenate(split(sheet), axis=0)
+        rows_freq = FINE * rows_back
+
+        def find(i):
+            span = pl.ds(pl.multiple_of(first_of(i) * LANES, wide * LANES), wide * LANES)
+            return dot(left, pick[:, span])
+
+        found = find(0)
+        for i in range(rounds):
+            following = find(i + 1) if i + 1 < rounds else None
+            for k in range(wide):
+                here = jnp.broadcast_to(fines[first_of(i) + k], (8, LANES)) - sub_of
+                tile = jnp.zeros((8, LANES), F32)
+                for m in range(FINE // share_of):
+                    at = (slice(m * 8, (m + 1) * 8), slice(k * LANES, (k + 1) * LANES))
+                    block = found[:rows_freq][at] + found[rows_freq:][at]
+                    tile = tile + jnp.where(here == m * share_of, block, 0.0)
+                shift = 4
+                while shift >= rows_back:
+                    tile = tile + pltpu.roll(tile, shift, 0)
+                    shift //= 2
+                back[c, first_of(i) + k] = tile[0:rows_back]
+            if i > 0:
+                for step in range(wide):
+                    give(c, peer((rounds - i) * wide + wide - 1 - step))
+            found = following
+        for step in range(wide - 1):
+            give(c, peer(wide - 1 - step))
+        pltpu.make_async_copy(back.at[c, me], back_in.at[c, me], back_sem.at[c]).start()
+
     lane_half = lax.broadcasted_iota(jnp.int32, (half, 2 * half), 1)
     for c in range(layers // batch):
         pltpu.make_async_copy(pot_in.at[c], pot_in.at[c], pot_sem.at[c]).wait()
@@ -374,46 +430,9 @@
                 for h in range(halves):
                     sides = [block[q * FINE : (q + 1) * FINE] for q in range(h * per, (h + 1) * per)]
                     line = jnp.concatenate(sides, axis=1)
-                    at = part * layers + c * batch + i
-                    mesh[h, pl.ds(at, FINE, stride=rows_msg), :] = line
-
-    wide = 4
-    rounds = count // wide
-    left = jnp.concatenate(split(jnp.concatenate([mesh[h] for h in range(halves)], axis=1)), axis=0)
-
-    def give(other):
-        pltpu.make_async_remote_copy(
-            src_ref=back.at[other],
-            dst_ref=back_in.at[me],
-            send_sem=send_sem.at[3],
-            recv_sem=recv_sem.at[3],
-            device_id={"ga": other},
-        ).start()
-
-    def first_of(i):
-        return lax.div(peer((rounds - 1 - i) * wide), wide) * wide
-
-    def find(i):
-        span = pl.ds(pl.multiple_of(first_of(i) * LANES, wide * LANES), wide * LANES)
-        return dot(left, pick[:, span])
-
-    found = find(0)
-    for i in range(rounds):
-        following = find(i + 1) if i + 1 < rounds else None
-        for k in range(wide):
-            here = jnp.broadcast_to(fines[first_of(i) + k], (rows_msg, LANES))
-            tile = jnp.zeros((rows_msg, LANES), F32)
-            for f in range(FINE):
-                cut = (slice(f * rows_msg, (f + 1) * rows_msg), slice(k * LANES, (k + 1) * LANES))
-                tile = tile + jnp.where(here == f, found[:rows_mesh][cut] + found[rows_mesh:][cut], 0.0)
-            back[first_of(i) + k] = tile
-        if i > 0:
-            for step in range(wide):
-                give(peer((rounds - i) * wide + wide - 1 - step))
-        found = following
-    for step in range(wide - 1):
-        give(peer(wide - 1 - step))
-    pltpu.make_async_copy(back.at[me], back_in.at[me], recv_sem.at[3]).start()
+                    freq[c, h, pl.ds(part * batch + i, FINE, stride=rows_back), :] = line
+        take(c)
+
     rest.wait()
 
     def add(t, carry):
@@ -423,10 +442,11 @@
 
     lax.fori_loop(0, bands_all // 16, add, 0)
     load_last.wait()
-    arrive(back_in, 3)
+    for c in range(layers // batch):
+        pltpu.make_async_copy(back_in.at[c], back_in.at[c], back_sem.at[c]).wait()
 
     sub_half = lax.broadcasted_iota(jnp.int32, (half, LANES), 0).astype(F32)
-    final = dot(last_ref[...], stacked(back_in[...].reshape(count * rows_msg, LANES), 0))
+    final = dot(last_ref[...], stacked(back_in[...].reshape(parts * count, LANES), 0))
     high, low = split(final)
     final_cat = jnp.concatenate([high, low], axis=1)
     place_rows = jnp.concatenate([place[...], place[...]], axis=0)
@@ -488,7 +508,11 @@
         return carry
 
     sweep(0, 0)
-    lax.fori_loop(1, spans, sub_step, 0)
+    lax.fori_loop(1, spans - 1, sub_step, 0)
+    narrow(spans - 2, (spans - 2) % 2)
+    for other in share(spans - 2):
+        publish(spans - 2, other)
+    sweep(spans - 1, (spans - 1) % 2)
     narrow(spans - 1, (spans - 1) % 2)
     for other in share(spans - 1)[:-1]:
         publish(spans - 1, other)
@@ -504,7 +528,8 @@
     sent(msg, 1)
     for c in range(layers // batch):
         sent(pot_out.at[c], 2)
-    sent(back, 3)
+    for c in range(layers // batch):
+        sent(back.at[c], 3)
     sub_view = sub_in.at[pl.ds(0, count - 1)]
     pltpu.make_async_copy(sub_view, sub_view, send_sem.at[4]).wait()
 
@@ -528,7 +553,7 @@
     narrow = int(is_narrow(extent, count, parts))
     batch = min(2, layers)
     folds = half // FINE
-    constants = [jnp.asarray(t) for t in tables(extent, count, rows_msg)]
+    constants = [jnp.asarray(t) for t in tables(extent, count, rows_msg, batch)]
     vmem = pl.BlockSpec(memory_space=pltpu.VMEM)
     staged = [(blocks, LANES), (layers, extent, extent)] + [t.shape for t in constants]
     kinds = [jnp.int32, F32] + [BF] * len(constants)
@@ -545,8 +570,9 @@
         pltpu.VMEM((count, 1, LANES), F32),
         pltpu.VMEM((2 * FINE * rows_msg, folds * half), F32),
         pltpu.VMEM((folds * half // LANES, FINE * rows_msg, LANES), F32),
-        pltpu.VMEM((count, rows_msg, LANES), F32),
-        pltpu.VMEM((count, rows_msg, LANES), F32),
+        pltpu.VMEM((layers // batch, folds * half // LANES, FINE * 2 * batch, LANES), F32),
+        pltpu.VMEM((layers // batch, count, 2 * batch, LANES), F32),
+        pltpu.VMEM((layers // batch, count, 2 * batch, LANES), F32),
         pltpu.VMEM((2, 2, 64, LANES), F32),
         pltpu.VMEM((bands_all // 64, 1, LANES), F32),
         pltpu.VMEM((count, 1, LANES), F32),
@@ -562,6 +588,7 @@
         pltpu.SemaphoreType.DMA((5,)),
         pltpu.SemaphoreType.DMA((count // group,)),
         pltpu.SemaphoreType.DMA((count // group,)),
+        pltpu.SemaphoreType.DMA((layers // batch,)),
         pltpu.SemaphoreType.DMA((layers // batch,)),
     ]
     applied, sub = pl.pallas_call(

time: 32.4 us -> 32.3 us (level)
  no operation moved by 1% of the time
where the time goes in v4:
time: 32.3 us; the launch traced here: 32.1 us
  Pallas kernels  31.4 us (97%)
  between operations  0.64 us (2%)
    pallas_call x1, Pallas kernels, local(): pl.pallas_call(functools.partial(kernel, count, layers, extent, rows_msg,...  30.8 us

profile of v4, /device:TPU:0, one launch (start us, length us, event | category | flops | bytes accessed | tf_op | source)
XLA Modules:
  0.0 32.1 jit_solution(13961867294554193646)
XLA Ops:
  0.6 30.8 %shard_map.104 = (f32[2,32,128]{2,1,0:T(8,128)S(1)}, f32[2,1,32]{2,1,0:T(1,128)S(1)}) custom-call(s32[32,128]{1,0:T(8,128)} %bitcast.3, f32[4,128,128]{2,1,0:T(8,128)} %pot_hbm.1, bf16[256,384]{1,0:T(8,128)(2,1)} %constant.12.clone.first_hbm, bf16[256,384]{1,0:T(8,128)(2,1)} %constant.13.clone.up_a_hbm, bf16[256,256]{1,0:T(8,128)(2,1)} %constant.14.clone.up_b_hbm, ...), custom_call_target="tpu_custom_call" | custom-call | tf_op jit(solution)/shard_map/pallas_call | solution.py:594
  31.5 0.6 %shard_map.105 = (f32[2,32,128]{2,1,0:T(8,128)}, f32[2,1,32]{2,1,0:T(1,128)}) custom-call(f32[2,32,128]{2,1,0:T(8,128)S(1)} %get-tuple-element.6.applied_ref, f32[2,1,32]{2,1,0:T(1,128)S(1)} %get-tuple-element.7.sub_ref), custom_call_target="tpu_custom_call" | custom-call | tf_op jit(solution)/shard_map/pallas_call | solution.py:607
